TPU v7x, 32 devices: a whole 2x2x4 slice. The times are simulated.
32 devices in a mesh: groups: 2 (over y), rows: 4 (over z), cols: 2 (over x), sub: 2 (over core).
Axes of the slice: x: 2, y: 2, z: 4, core: 2. Of those that a mesh axis runs over, the one named last changes fastest.
Arguments:
- diagonal_tiles: float32 [256, 128, 128], P(('groups', 'rows', 'sub')), parts along dimension 0
- coupling_tiles: float32 [256, 6, 128, 128], P(('groups', 'rows', 'sub'), 'cols'), parts along dimension 0, may hold values from -0.0625 to 0.0625
- column_part: int32 [256, 6], P(('groups', 'rows', 'sub'), 'cols'), parts along dimension 0, may hold values from 0 to 4
- column_tile: int32 [256, 6], P(('groups', 'rows', 'sub'), 'cols'), parts along dimension 0, may hold values from 0 to 31
- neighbours: int32 [8, 4], P('groups'), parts along dimension 0, may hold values from 0 to 3, as said below
- right_side: float32 [256, 128], P(('groups', 'rows', 'sub')), parts along dimension 0, may hold values from -6 to 6
- jacobi_inverse: float32 [256, 128, 128], P(('groups', 'rows', 'sub')), parts along dimension 0, as said below
Outputs:
- solution: float32 [256, 128], P(('groups', 'rows', 'sub')), parts along dimension 0
- residual: float32 [256, 128], P(('groups', 'rows', 'sub')), parts along dimension 0
There are 2 independent parts, one for each index of `groups`. A program takes and returns all parts, laid end to end along the dimension named above; each array names one. Nothing has to cross between parts.
Inputs may be any that keep to these rules, and one draw needn't show every extreme that they name: `neighbours`: entry 0 of partition p's list is (p + 4 // 2) mod 4, the opposite partition on the cycle; every other entry names a partition whose index differs from p by 1 to 2 (without wrapping round); entries may repeat. `jacobi_inverse`: block-diagonal: each group of 5 consecutive variables, from the first on, forms one 5 x 5 block, and each variable left over after the last whole group of 5 is a 1 x 1 block of its own.
All inputs are finite; a program needn't handle non-finite values.
Results may differ from a plain program's by a relative error of at most 0.00019.
Values sent between devices are 32-bit elements; how exact they have to be, the bound alone decides.
A program may use at most 64 MiB of HBM per device.

v0:
```python
import jax
import jax.numpy as jnp
from jax import lax
from jax.sharding import PartitionSpec as P

ITERS = 2


def transpose_apply(vector, diagonal_tiles, coupling_tiles, column_part, column_tile, neighbours):
    highest = lax.Precision.HIGHEST
    diagonal_part = jnp.einsum("rij,ri->rj", diagonal_tiles, vector, precision=highest)
    partial_value = jnp.einsum("rkij,ri->rkj", coupling_tiles, vector, precision=highest)
    tile_width = vector.shape[1]
    partial_value = partial_value.reshape(-1, tile_width)
    rows_dev = vector.shape[0]
    sub_count = lax.axis_size("sub")
    part_rows = rows_dev * sub_count
    own_part = lax.axis_index("rows")
    listed = neighbours[own_part]
    chosen = listed[jnp.maximum(column_part - 1, 0)]
    target = jnp.where(column_part == 0, own_part, chosen)
    landing = (target * part_rows + column_tile).reshape(-1)
    row_ids = lax.iota(jnp.int32, rows_dev * lax.axis_size(("rows", "sub")))
    one_hot = (row_ids[:, None] == landing[None, :]).astype(jnp.float32)
    owned = lax.psum_scatter(
        jnp.dot(one_hot, partial_value, precision=highest, preferred_element_type=jnp.float32),
        ("rows", "sub"),
        scatter_dimension=0,
        tiled=True,
    )
    owned = lax.psum(owned, "cols")
    return diagonal_part + owned


def precondition(jacobi_inverse, vector):
    return jnp.einsum("rij,ri->rj", jacobi_inverse, vector, precision=lax.Precision.HIGHEST)


def on_device(
    diagonal_tiles, coupling_tiles, column_part, column_tile, neighbours, right_side, jacobi_inverse
):

    def apply_a(vector):
        return transpose_apply(
            vector, diagonal_tiles, coupling_tiles, column_part, column_tile, neighbours
        )

    solution = jnp.zeros_like(right_side)
    residual = right_side
    search = right_side
    rho_now = lax.psum(jnp.sum(right_side * residual), ("rows", "sub"))
    for step in range(ITERS):
        search_hat = precondition(jacobi_inverse, search)
        image = apply_a(search_hat)
        alpha = rho_now / lax.psum(jnp.sum(right_side * image), ("rows", "sub"))
        half = residual - alpha * image
        half_hat = precondition(jacobi_inverse, half)
        twice = apply_a(half_hat)
        cross, square, shadow_half, shadow_twice = lax.psum(
            (
                jnp.sum(twice * half),
                jnp.sum(twice * twice),
                jnp.sum(right_side * half),
                jnp.sum(right_side * twice),
            ),
            ("rows", "sub"),
        )
        omega = cross / square
        solution = solution + alpha * search_hat + omega * half_hat
        residual = half - omega * twice
        if step + 1 < ITERS:
            rho_next = shadow_half - omega * shadow_twice
            search = residual + rho_next / rho_now * (alpha / omega) * (search - omega * image)
            rho_now = rho_next
    return (solution, residual)


def solution(mesh):
    in_specs = (
        P(("groups", "rows", "sub"), None, None),
        P(("groups", "rows", "sub"), "cols", None, None),
        P(("groups", "rows", "sub"), "cols"),
        P(("groups", "rows", "sub"), "cols"),
        P("groups", None),
        P(("groups", "rows", "sub"), None),
        P(("groups", "rows", "sub"), None, None),
    )
    out_specs = (P(("groups", "rows", "sub"), None), P(("groups", "rows", "sub"), None))
    return jax.shard_map(
        on_device, mesh=mesh, in_specs=in_specs, out_specs=out_specs, check_vma=False
    )
```

profile of v0, /device:TPU:0, one launch (start us, length us, event | category | flops | bytes accessed | tf_op | source)
XLA Modules:
  0.0 245.4 jit_solution(2506493067648481065)
XLA Ops:
  10.0 2.2 fusion.24
  12.2 1.9 fusion.20
  15.0 2.2 fusion.22
  17.2 31.2 %reduce-scatter.5.cloned.1.call-done = f32[16,128]{1,0:T(8,128)} async-done(((f32[128,128]{1,0:T(8,128)}), f32[16,128]{1,0:T(8,128)}) %reduce-scatter.5.cloned.1.call-update) | async-done | bytes 8208 | tf_op jit(solution)/shard_map/reduce_scatter | solution.py:25
  48.4 5.1 %psum.92 = f32[16,128]{1,0:T(8,128)S(1)} all-reduce(f32[16,128]{1,0:T(8,128)} %reduce-scatter.5.cloned.1.call-done), channel_id=1, replica_groups=mesh['groups'=2,'rows'=4,'cols'=2,'sub'=2] {'cols'}, use_global_device_ids=true, to_apply=%region_3.4 | all-reduce | flops 2048 | bytes 16384 | tf_op jit(solution)/shard_map/psum | solution.py:31
  54.1 14.2 %all-reduce.2 = (f32[]{:T(128)}, f32[]{:T(128)}) all-reduce(f32[]{:T(128)} %get-tuple-element.9, f32[]{:T(128)} %get-tuple-element.8), channel_id=1, replica_groups=mesh['groups'=2,'rows'=4,'cols'=2,'sub'=2] {'rows','sub'}, use_global_device_ids=true, to_apply=%region_1.0 | all-reduce | flops 2 | bytes 16 | tf_op jit(solution)/shard_map/psum | solution.py:51
  69.6 2.2 fusion.25
  71.8 1.9 fusion.16
  74.6 2.2 fusion.18
  76.8 26.5 %reduce-scatter.7.cloned.1.call-done = f32[16,128]{1,0:T(8,128)} async-done(((f32[128,128]{1,0:T(8,128)}), f32[16,128]{1,0:T(8,128)}) %reduce-scatter.7.cloned.1.call-update) | async-done | bytes 8208 | tf_op jit(solution)/shard_map/reduce_scatter | solution.py:25
  103.2 5.1 %psum.94 = f32[16,128]{1,0:T(8,128)S(1)} all-reduce(f32[16,128]{1,0:T(8,128)} %reduce-scatter.7.cloned.1.call-done), channel_id=1, replica_groups=mesh['groups'=2,'rows'=4,'cols'=2,'sub'=2] {'cols'}, use_global_device_ids=true, to_apply=%region_7.8 | all-reduce | flops 2048 | bytes 16384 | tf_op jit(solution)/shard_map/psum | solution.py:31
  109.0 14.3 %all-reduce.1 = (f32[]{:T(128)}, f32[]{:T(128)}, f32[]{:T(128)}, f32[]{:T(128)}) all-reduce(f32[]{:T(128)} %get-tuple-element.7, f32[]{:T(128)} %get-tuple-element.6, f32[]{:T(128)} %get-tuple-element.5, f32[]{:T(128)} %get-tuple-element.4), channel_id=1, replica_groups=mesh['groups'=2,'rows'=4,'cols'=2,'sub'=2] {'rows','sub'}, use_global_device_ids=true, to_apply=%region_13.14 | all-reduce | flops 4 | bytes 32 | tf_op jit(solution)/shard_map/psum | solution.py:59
  129.0 2.2 fusion.26
  131.2 1.9 fusion.12
  134.2 2.2 fusion.14
  136.3 26.4 %reduce-scatter.9.cloned.1.call-done = f32[16,128]{1,0:T(8,128)} async-done(((f32[128,128]{1,0:T(8,128)}), f32[16,128]{1,0:T(8,128)}) %reduce-scatter.9.cloned.1.call-update) | async-done | bytes 8208 | tf_op jit(solution)/shard_map/reduce_scatter | solution.py:25
  162.7 5.1 %psum.99 = f32[16,128]{1,0:T(8,128)S(1)} all-reduce(f32[16,128]{1,0:T(8,128)} %reduce-scatter.9.cloned.1.call-done), channel_id=1, replica_groups=mesh['groups'=2,'rows'=4,'cols'=2,'sub'=2] {'cols'}, use_global_device_ids=true, to_apply=%region_17.18 | all-reduce | flops 2048 | bytes 16384 | tf_op jit(solution)/shard_map/psum | solution.py:31
  168.4 14.2 %psum.100 = f32[]{:T(128)} all-reduce(f32[]{:T(128)} %get-tuple-element.19), channel_id=1, replica_groups=mesh['groups'=2,'rows'=4,'cols'=2,'sub'=2] {'rows','sub'}, use_global_device_ids=true, to_apply=%region_19.20 | all-reduce | flops 1 | bytes 8 | tf_op jit(solution)/shard_map/psum | solution.py:55
  183.3 2.2 fusion.27
  185.5 1.9 fusion.8
  188.2 2.2 fusion.10
  190.4 26.6 %reduce-scatter.11.cloned.1.call-done = f32[16,128]{1,0:T(8,128)} async-done(((f32[128,128]{1,0:T(8,128)}), f32[16,128]{1,0:T(8,128)}) %reduce-scatter.11.cloned.1.call-update) | async-done | bytes 8208 | tf_op jit(solution)/shard_map/reduce_scatter | solution.py:25
  217.0 5.1 %psum.101 = f32[16,128]{1,0:T(8,128)S(1)} all-reduce(f32[16,128]{1,0:T(8,128)} %reduce-scatter.11.cloned.1.call-done), channel_id=1, replica_groups=mesh['groups'=2,'rows'=4,'cols'=2,'sub'=2] {'cols'}, use_global_device_ids=true, to_apply=%region_21.22 | all-reduce | flops 2048 | bytes 16384 | tf_op jit(solution)/shard_map/psum | solution.py:31
  222.7 14.2 %all-reduce = (f32[]{:T(128)}, f32[]{:T(128)}) all-reduce(f32[]{:T(128)} %get-tuple-element.3, f32[]{:T(128)} %get-tuple-element.2), channel_id=1, replica_groups=mesh['groups'=2,'rows'=4,'cols'=2,'sub'=2] {'rows','sub'}, use_global_device_ids=true, to_apply=%region_23.24 | all-reduce | flops 2 | bytes 16 | tf_op jit(solution)/shard_map/psum | solution.py:59
  (44 shorter events, 9.5 us)
Async XLA Ops:
  7.2 5.1 %copy-start = (f32[16,3,128,128]{3,2,1,0:T(8,128)S(1)}, f32[16,3,128,128]{3,2,1,0:T(8,128)}, u32[]{:S(2)}) copy-start(f32[16,3,128,128]{3,2,1,0:T(8,128)} %param.8) | copy-start | bytes 9437188
  7.2 41.2 %reduce-scatter.5.cloned.1.call-start = ((), (), s32[]{:S(2)}) async-start(), calls=%async_computation.4 | async-start | bytes 73728 | tf_op jit(solution)/shard_map/reduce_scatter | solution.py:25
  8.9 0.9 copy-start.2
  8.9 1.1 copy-start.1
  14.9 88.3 %reduce-scatter.7.cloned.1.call-start = ((), (), s32[]{:S(2)}) async-start(), calls=%async_computation.5 | async-start | bytes 73728 | tf_op jit(solution)/shard_map/reduce_scatter | solution.py:25
  74.5 88.2 %reduce-scatter.9.cloned.1.call-start = ((), (), s32[]{:S(2)}) async-start(), calls=%async_computation.6 | async-start | bytes 73728 | tf_op jit(solution)/shard_map/reduce_scatter | solution.py:25
  133.9 83.1 %reduce-scatter.11.cloned.1.call-start = ((), (), s32[]{:S(2)}) async-start(), calls=%async_computation.7 | async-start | bytes 73728 | tf_op jit(solution)/shard_map/reduce_scatter | solution.py:25
Sparse Core Ops, SparseCore 0:
  15.1 33.2 reduce-scatter.4
  74.7 28.5 reduce-scatter.6
  134.0 28.6 reduce-scatter.8
  188.4 28.6 reduce-scatter.10
where the time goes:
time: 246 us; the launch traced here: 245 us
  waiting for transfers between devices  111 us (45%)
  blocking collectives  77.3 us (31%)
  matrix products  28.1 us (11%)
  between operations  23 us (9%)
  other arithmetic  3.16 us (1%)
  local copies, waits for them, and re-layouts  2.84 us (1%)
    reduce_scatter x4, waiting for transfers between devices, transpose_apply(): lax.psum_scatter(jnp.dot(one_hot, partial_value, precision=highest, prefe...  111 us
    psum x2, blocking collectives, on_device(): lax.psum((jnp.sum(twice * half), jnp.sum(twice * twice), jnp.sum(right_si...  28.5 us
    psum x4, blocking collectives, transpose_apply(): owned = lax.psum(owned, 'cols')  20.3 us
    psum x1, blocking collectives, on_device(): rho_now = lax.psum(jnp.sum(right_side * residual), ('rows', 'sub'))  14.2 us
    psum x1, blocking collectives, on_device(): alpha = rho_now / lax.psum(jnp.sum(right_side * image), ('rows', 'sub'))  14.2 us
    dot_general x4, matrix products, precondition(): jnp.einsum('rij,ri->rj', jacobi_inverse, vector, precision=lax.Precision....  8.77 us
    dot_general x4, matrix products, transpose_apply(): jnp.einsum('rij,ri->rj', diagonal_tiles, vector, precision=highest)  8.74 us
    dot_general x4, matrix products, transpose_apply(): jnp.einsum('rkij,ri->rkj', coupling_tiles, vector, precision=highest)  7.46 us
  transfers between devices with their start and end apart: 4, of which 4 were waited for; matrix products, arithmetic and copies ran while one was open for 4% of the time, Pallas kernels for 0%

commit v1 on v0

v1 whole, which is shorter than its diff:
```python
import functools

import jax
import jax.numpy as jnp
from jax import lax
from jax.experimental import pallas as pl
from jax.experimental.pallas import tpu as pltpu
from jax.sharding import PartitionSpec as P

MESH = pl.DeviceIdType.MESH
REACH = 2
APPLIES = 4
SUBLANES = 8
F32 = jnp.float32


def offsets_of(count):
    wanted = {d % count for d in range(-REACH, REACH + 1)} | {count // 2}
    return sorted(wanted)


def kernel(
    sizes,
    diag_hbm,
    coup_hbm,
    jac_hbm,
    part_ref,
    tile_ref,
    near_ref,
    right_ref,
    sol_ref,
    res_ref,
    diag,
    coup,
    jac,
    one_hot,
    prod,
    dprod,
    vec,
    landed,
    pair_recv,
    owned,
    recv,
    dots,
    dots_recv,
    load_sem,
    pair_send_sem,
    pair_recv_sem,
    send_sem,
    recv_sem,
    dots_send_sem,
    dots_recv_sem,
):
    n_rows, n_cols, n_sub = sizes
    offsets = offsets_of(n_rows)
    slots = len(offsets)
    rows_dev, slot_count, width, _ = coup.shape
    half_rows = slots * rows_dev
    chunk = rows_dev * SUBLANES
    row = lax.axis_index("rows")
    col = lax.axis_index("cols")
    sub = lax.axis_index("sub")
    me = row * n_sub + sub
    twin = n_sub - 1 - sub

    loads = [
        pltpu.make_async_copy(jac_hbm, jac, load_sem.at[0]),
        pltpu.make_async_copy(diag_hbm, diag, load_sem.at[1]),
        pltpu.make_async_copy(coup_hbm, coup, load_sem.at[2]),
    ]
    for load in loads:
        load.start()

    def partner(slot):
        return lax.rem(row + offsets[slot], n_rows)

    def if_linked(slot, act):
        if offsets[slot] in (0, n_rows // 2):
            act()
        else:
            pl.when(jnp.abs(partner(slot) - row) <= REACH)(act)

    barrier = pltpu.get_barrier_semaphore()

    def dot_peers():
        for step in range(1, n_rows * n_sub):
            peer = lax.rem(me + step, n_rows * n_sub)
            yield step, peer, {"rows": lax.div(peer, n_sub), "cols": col, "sub": lax.rem(peer, n_sub)}

    recv[...] = jnp.zeros_like(recv)
    dots[...] = jnp.zeros_like(dots)
    for _, _, where in dot_peers():
        pl.semaphore_signal(barrier, inc=1, device_id=where, device_id_type=MESH)
    for slot in range(slots):
        for step in range(1, n_cols):
            where = {"rows": partner(slot), "cols": lax.rem(col + step, n_cols), "sub": sub}

            def greet(where=where):
                pl.semaphore_signal(barrier, inc=1, device_id=where, device_id_type=MESH)

            if_linked(slot, greet)

    part = part_ref[...]
    tile = tile_ref[...]
    target = jnp.full(part.shape, row, jnp.int32)
    for j in range(near_ref.shape[1]):
        target = jnp.where(part == j + 1, near_ref[row, j], target)
    apart = target - row
    apart = jnp.where(apart < 0, apart + n_rows, apart)
    place = jnp.zeros(part.shape, jnp.int32)
    for slot in range(1, slots):
        place = jnp.where(apart == offsets[slot], slot, place)
    landing = place * rows_dev + tile
    for j in range(1, n_sub):
        landing = jnp.where(tile >= j * rows_dev, landing + (half_rows - rows_dev), landing)
    lanes = -(-n_sub * half_rows // 128) * 128
    lane = lax.broadcasted_iota(jnp.int32, (rows_dev, lanes), 1)
    for k in range(slot_count):
        hit = (landing[:, k : k + 1] == lane).astype(F32)
        hit = jnp.broadcast_to(hit[:, None, :], (rows_dev, SUBLANES, lanes)).reshape(chunk, lanes)
        turned = jnp.transpose(hit)[: n_sub * half_rows]
        one_hot[:, k * chunk : (k + 1) * chunk] = turned.astype(jnp.bfloat16)

    loads[0].wait()

    def turn(r, carry):
        jac[r] = jnp.transpose(jac[r])
        return carry

    lax.fori_loop(0, rows_dev, turn, 0, unroll=4)

    def pair_copy(e):
        return pltpu.make_async_remote_copy(
            src_ref=landed.at[e, pl.ds(pl.multiple_of(twin * half_rows, rows_dev), half_rows)],
            dst_ref=pair_recv.at[e],
            send_sem=pair_send_sem.at[e],
            recv_sem=pair_recv_sem.at[e],
            device_id={"sub": twin},
            device_id_type=MESH,
        )

    def owner_copy(e, slot, step):
        back = offsets.index(-offsets[slot] % n_rows)
        return pltpu.make_async_remote_copy(
            src_ref=owned.at[e, pl.ds(slot * rows_dev, rows_dev)],
            dst_ref=recv.at[e, back, col],
            send_sem=send_sem.at[e, slot, step],
            recv_sem=recv_sem.at[e, back, col],
            device_id={"rows": partner(slot), "cols": lax.rem(col + step, n_cols)},
            device_id_type=MESH,
        )

    def owner_arrival(e, slot, step):
        source = lax.rem(col + step, n_cols)
        return pltpu.make_async_remote_copy(
            src_ref=owned.at[e, pl.ds(slot * rows_dev, rows_dev)],
            dst_ref=recv.at[e, slot, source],
            send_sem=send_sem.at[e, slot, step],
            recv_sem=recv_sem.at[e, slot, source],
            device_id={"rows": partner(slot), "cols": source},
            device_id_type=MESH,
        )

    routes = [(s, c) for s in range(slots) for c in range(n_cols) if (s, c) != (0, 0)]

    def each_route(act):
        for slot, step in routes:
            if_linked(slot, functools.partial(act, slot, step))

    def dots_copy(e, step, peer, where):
        return pltpu.make_async_remote_copy(
            src_ref=dots.at[e],
            dst_ref=dots_recv.at[e, me],
            send_sem=dots_send_sem.at[e, step],
            recv_sem=dots_recv_sem.at[e, me],
            device_id=where,
            device_id_type=MESH,
        )

    def dots_start(e, products):
        for j, product in enumerate(products):
            dots[e, j : j + 1] = jnp.sum(product, axis=0, keepdims=True)
        for step, peer, where in dot_peers():
            dots_copy(e, step, peer, where).start()
        dots_recv[e, me] = dots[e]

    def dots_finish(e, count):
        for step, peer, where in dot_peers():
            pltpu.make_async_remote_copy(
                src_ref=dots.at[e],
                dst_ref=dots_recv.at[e, peer],
                send_sem=dots_send_sem.at[e, step],
                recv_sem=dots_recv_sem.at[e, peer],
                device_id=where,
                device_id_type=MESH,
            ).wait_recv()
        total = jnp.sum(dots_recv[e], axis=0)
        total = jnp.broadcast_to(jnp.sum(total, axis=1, keepdims=True), total.shape)
        return [total[j : j + 1] for j in range(count)]

    def fold(product):
        return jnp.sum(product.reshape(width // SUBLANES, SUBLANES, width), axis=0)

    unroll = 4 if rows_dev % 4 == 0 else 1

    def apply(e, value):
        vec[e] = value
        if e == 0:
            loads[1].wait()
            loads[2].wait()

        def some_rows(g, carry):
            for u in range(unroll):
                r = g * unroll + u
                hat = jnp.sum(jac[r] * vec[e, pl.ds(r, 1)], axis=1, keepdims=True)
                hat = jnp.broadcast_to(hat, (width, width))
                for k in range(slot_count):
                    at = pl.multiple_of(k * chunk + r * SUBLANES, SUBLANES)
                    prod[pl.ds(at, SUBLANES)] = fold(coup[r, k] * hat)
                dprod[pl.ds(pl.multiple_of(r * SUBLANES, SUBLANES), SUBLANES)] = fold(diag[r] * hat)
            return carry

        lax.fori_loop(0, rows_dev // unroll, some_rows, 0)
        rest = prod[...]
        out = None
        for _ in range(3):
            piece = rest.astype(jnp.bfloat16)
            rest = rest - piece.astype(F32)
            term = jnp.dot(one_hot[...], piece, preferred_element_type=F32)
            out = term if out is None else out + term
        landed[e] = out
        if e == 0:
            greetings = n_rows * n_sub - 1
            for slot in range(slots):
                linked = 1
                if offsets[slot] not in (0, n_rows // 2):
                    linked = (jnp.abs(partner(slot) - row) <= REACH).astype(jnp.int32)
                greetings = greetings + (n_cols - 1) * linked
            pl.semaphore_wait(barrier, greetings)
        pair_copy(e).start()
        pair_copy(e).wait_recv()
        mine = landed[e, pl.ds(pl.multiple_of(sub * half_rows, rows_dev), half_rows)]
        owned[e] = mine + pair_recv[e]
        each_route(lambda slot, step: owner_copy(e, slot, step).start())
        recv[e, 0, col] = owned[e, :rows_dev]
        own = jnp.sum(dprod[...].reshape(rows_dev, SUBLANES, width), axis=1)
        each_route(lambda slot, step: owner_arrival(e, slot, step).wait_recv())
        for slot in range(slots):
            for c in range(n_cols):
                own = own + recv[e, slot, c]
        return own

    shadow = right_ref[...]
    image = apply(0, shadow)
    dots_start(0, [shadow * shadow, shadow * image])
    second = apply(1, image)
    rho, shadow_image = dots_finish(0, 2)
    alpha = rho / shadow_image
    half = shadow - alpha * image
    twice = image - alpha * second
    dots_start(1, [twice * half, twice * twice, shadow * half, shadow * twice])
    third = apply(2, twice)
    cross, square, shadow_half, shadow_twice = dots_finish(1, 4)
    omega = cross / square
    rho_next = shadow_half - omega * shadow_twice
    beta = rho_next / rho * (alpha / omega)
    residual = half - omega * twice
    search = residual + beta * (shadow - omega * image)
    residual_image = twice - omega * third
    image = residual_image + beta * (image - omega * second)
    dots_start(2, [shadow * image])
    fourth = apply(3, image)
    alpha_next = rho_next / dots_finish(2, 1)[0]
    half_next = residual - alpha_next * image
    twice = residual_image - alpha_next * fourth
    dots_start(3, [twice * half_next, twice * twice])

    vec[0] = alpha * shadow + omega * half + alpha_next * search
    vec[1] = half_next
    at_lane = lax.broadcasted_iota(jnp.int32, (width, width), 1)

    def hats(r, carry):
        for j in range(2):
            hat = jnp.sum(jac[r] * vec[j, pl.ds(r, 1)], axis=1, keepdims=True)
            carry = jnp.where(at_lane == j * rows_dev + r, hat, carry)
        return carry

    hat = lax.fori_loop(0, rows_dev, hats, jnp.zeros((width, width), F32), unroll=4)
    hat = jnp.transpose(hat)
    cross, square = dots_finish(3, 2)
    omega = cross / square
    sol_ref[...] = hat[:rows_dev] + omega * hat[rows_dev : 2 * rows_dev]
    res_ref[...] = half_next - omega * twice

    for e in range(APPLIES):
        pair_copy(e).wait_send()
        each_route(lambda slot, step: owner_copy(e, slot, step).wait_send())
        for step, peer, where in dot_peers():
            dots_copy(e, step, peer, where).wait_send()


def on_device(
    diagonal_tiles, coupling_tiles, column_part, column_tile, neighbours, right_side, jacobi_inverse
):
    n_rows, n_cols, n_sub = (lax.axis_size(a) for a in ("rows", "cols", "sub"))
    slots = len(offsets_of(n_rows))
    rows_dev, slot_count, width, _ = coupling_tiles.shape
    half_rows = slots * rows_dev
    chunk = rows_dev * SUBLANES
    peers = n_rows * n_sub
    hbm = pl.BlockSpec(memory_space=pl.ANY)
    vmem = pl.BlockSpec(memory_space=pltpu.VMEM)
    dma = pltpu.SemaphoreType.DMA
    scratch = [
        pltpu.VMEM(diagonal_tiles.shape, F32),
        pltpu.VMEM(coupling_tiles.shape, F32),
        pltpu.VMEM(jacobi_inverse.shape, F32),
        pltpu.VMEM((n_sub * half_rows, slot_count * chunk), jnp.bfloat16),
        pltpu.VMEM((slot_count * chunk, width), F32),
        pltpu.VMEM((chunk, width), F32),
        pltpu.VMEM((APPLIES, rows_dev, width), F32),
        pltpu.VMEM((APPLIES, n_sub * half_rows, width), F32),
        pltpu.VMEM((APPLIES, half_rows, width), F32),
        pltpu.VMEM((APPLIES, half_rows, width), F32),
        pltpu.VMEM((APPLIES, slots, n_cols, rows_dev, width), F32),
        pltpu.VMEM((APPLIES, SUBLANES, width), F32),
        pltpu.VMEM((APPLIES, peers, SUBLANES, width), F32),
        dma((3,)),
        dma((APPLIES,)),
        dma((APPLIES,)),
        dma((APPLIES, slots, n_cols)),
        dma((APPLIES, slots, n_cols)),
        dma((APPLIES, peers)),
        dma((APPLIES, peers)),
    ]
    out = jax.ShapeDtypeStruct(right_side.shape, F32)
    return pl.pallas_call(
        functools.partial(kernel, (n_rows, n_cols, n_sub)),
        out_shape=(out, out),
        in_specs=[hbm, hbm, hbm, vmem, vmem, pl.BlockSpec(memory_space=pltpu.SMEM), vmem],
        out_specs=(vmem, vmem),
        scratch_shapes=scratch,
        compiler_params=pltpu.CompilerParams(
            collective_id=0, has_side_effects=True, vmem_limit_bytes=56 * 2**20
        ),
        name="solve",
    )(diagonal_tiles, coupling_tiles, jacobi_inverse, column_part, column_tile, neighbours, right_side)


def solution(mesh):
    in_specs = (
        P(("groups", "rows", "sub"), None, None),
        P(("groups", "rows", "sub"), "cols", None, None),
        P(("groups", "rows", "sub"), "cols"),
        P(("groups", "rows", "sub"), "cols"),
        P("groups", None),
        P(("groups", "rows", "sub"), None),
        P(("groups", "rows", "sub"), None, None),
    )
    out_specs = (P(("groups", "rows", "sub"), None), P(("groups", "rows", "sub"), None))
    return jax.shard_map(
        on_device, mesh=mesh, in_specs=in_specs, out_specs=out_specs, check_vma=False
    )
```

time: 246 us -> 41 us (0.17)
  waiting for transfers between devices: 111 us -> 0 us
  blocking collectives: 77.3 us -> 0 us
  Pallas kernels: 0 us -> 34.7 us
  matrix products: 28.1 us -> 0 us
  between operations: 23 us -> 0.64 us
  other arithmetic: 3.16 us -> 0 us
  local copies, waits for them, and re-layouts: 2.84 us -> 5.3 us
    reduce_scatter x4 -> x0, waiting for transfers between devices: 111 us -> none  [transpose_apply(): lax.psum_scatter(jnp.dot(one_hot, partial_value, precision=highest, prefe...]
    psum x8 -> x0, blocking collectives: 77.3 us -> none  [the longest x2 28.5 us: on_device(): lax.psum((jnp.sum(twice * half), jnp.sum(twice * twice), jnp.sum(right_si...]
    pallas_call x0 -> x1, Pallas kernels: none -> 34.7 us  [on_device(): pl.pallas_call(functools.partial(kernel, (n_rows, n_cols, n_sub)), out_sh...]
    dot_general x16 -> x0, matrix products: 28.1 us -> none  [the longest x4 8.77 us: precondition(): jnp.einsum('rij,ri->rj', jacobi_inverse, vector, precision=lax.Precision....]
    unnamed x8 -> x4, local copies, waits for them, and re-layouts: 1.01 us -> 5.3 us
    reduce_sum x4 -> x0, other arithmetic: 2.5 us -> none  [the longest x2 1.21 us: on_device(): alpha = rho_now / lax.psum(jnp.sum(right_side * image), ('rows', 'sub'))]
  transfers between devices with their start and end apart: 4 -> 0, of which waited for: 4 -> 0; matrix products, arithmetic and copies ran while one was open for 4% -> 0% of each run, Pallas kernels for 0% -> 0%
where the time goes in v1:
time: 41 us; the launch traced here: 40.6 us
  Pallas kernels  34.7 us (85%)
  local copies, waits for them, and re-layouts  5.3 us (13%)
  between operations  0.64 us (2%)
    pallas_call x1, Pallas kernels, on_device(): pl.pallas_call(functools.partial(kernel, (n_rows, n_cols, n_sub)), out_sh...  34.7 us
    unnamed x4, local copies, waits for them, and re-layouts  5.3 us

profile of v1, /device:TPU:0, one launch (start us, length us, event | category | flops | bytes accessed | tf_op | source)
XLA Modules:
  0.0 40.6 jit_solution(5416658053392064343)
XLA Ops:
  0.6 1.4 %copy.9.part_ref = s32[16,3]{1,0:T(8,128)} copy(s32[16,3]{0,1:T(4,128)} %param.9) | data formatting | bytes 384 | tf_op args[2]
  2.0 1.4 %copy.10.tile_ref = s32[16,3]{1,0:T(8,128)} copy(s32[16,3]{0,1:T(4,128)} %param.10) | data formatting | bytes 384 | tf_op args[3]
  3.3 34.7 %solve.1 = (f32[16,128]{1,0:T(8,128)}, f32[16,128]{1,0:T(8,128)}) custom-call(f32[16,128,128]{2,1,0:T(8,128)} %diag_hbm.1, f32[16,3,128,128]{3,2,1,0:T(8,128)} %coup_hbm.1, f32[16,128,128]{2,1,0:T(8,128)} %jac_hbm.1, s32[16,3]{1,0:T(8,128)} %copy.9.part_ref, s32[16,3]{1,0:T(8,128)} %copy.10.tile_ref, s32[4,4]{1,0:T(4,128)} %near_ref.1, f32[16,128]{1,0:T(8,128)} %right_ref.1), custom_call_target="tpu_custom_call" | custom-call | tf_op jit(solution)/shard_map/solve/pallas_call | solution.py:337
  38.0 1.3 %copy.13 = f32[16,128]{1,0:T(8,128)} copy(f32[16,128]{1,0:T(8,128)} %get-tuple-element.4) | data formatting | bytes 16384
  39.3 1.3 %copy.14 = f32[16,128]{1,0:T(8,128)} copy(f32[16,128]{1,0:T(8,128)} %get-tuple-element.5) | data formatting | bytes 16384

commit v2 on v1

--- a/solution.py
+++ b/solution.py
@@ -28,8 +28,7 @@
     tile_ref,
     near_ref,
     right_ref,
-    sol_ref,
-    res_ref,
+    out_ref,
     diag,
     coup,
     jac,
@@ -38,14 +37,10 @@
     dprod,
     vec,
     landed,
-    pair_recv,
-    owned,
     recv,
     dots,
     dots_recv,
     load_sem,
-    pair_send_sem,
-    pair_recv_sem,
     send_sem,
     recv_sem,
     dots_send_sem,
@@ -61,7 +56,6 @@
     col = lax.axis_index("cols")
     sub = lax.axis_index("sub")
     me = row * n_sub + sub
-    twin = n_sub - 1 - sub
 
     loads = [
         pltpu.make_async_copy(jac_hbm, jac, load_sem.at[0]),
@@ -80,6 +74,13 @@
         else:
             pl.when(jnp.abs(partner(slot) - row) <= REACH)(act)
 
+    def corner(slot, step):
+        return {
+            "rows": partner(slot),
+            "cols": lax.rem(col + step // n_sub, n_cols),
+            "sub": lax.rem(sub + step % n_sub, n_sub),
+        }
+
     barrier = pltpu.get_barrier_semaphore()
 
     def dot_peers():
@@ -88,14 +89,13 @@
             yield step, peer, {"rows": lax.div(peer, n_sub), "cols": col, "sub": lax.rem(peer, n_sub)}
 
     recv[...] = jnp.zeros_like(recv)
-    dots[...] = jnp.zeros_like(dots)
     for _, _, where in dot_peers():
         pl.semaphore_signal(barrier, inc=1, device_id=where, device_id_type=MESH)
     for slot in range(slots):
-        for step in range(1, n_cols):
-            where = {"rows": partner(slot), "cols": lax.rem(col + step, n_cols), "sub": sub}
-
-            def greet(where=where):
+        for step in range(n_sub, n_cols * n_sub):
+
+            def greet(slot=slot, step=step):
+                where = corner(slot, step)
                 pl.semaphore_signal(barrier, inc=1, device_id=where, device_id_type=MESH)
 
             if_linked(slot, greet)
@@ -113,13 +113,17 @@
     landing = place * rows_dev + tile
     for j in range(1, n_sub):
         landing = jnp.where(tile >= j * rows_dev, landing + (half_rows - rows_dev), landing)
-    lanes = -(-n_sub * half_rows // 128) * 128
-    lane = lax.broadcasted_iota(jnp.int32, (rows_dev, lanes), 1)
+    from_row = lax.broadcasted_iota(jnp.int32, (rows_dev, chunk), 0)
+    to_lane = lax.broadcasted_iota(jnp.int32, (rows_dev, chunk), 1)
+    first = from_row * SUBLANES
+    spread = ((to_lane >= first) & (to_lane < first + SUBLANES)).astype(F32)
+    spread_landing = jnp.dot(
+        landing.astype(F32), spread, precision=lax.Precision.HIGHEST, preferred_element_type=F32
+    )
+    at_row = lax.broadcasted_iota(jnp.int32, (n_sub * half_rows, chunk), 0).astype(F32)
     for k in range(slot_count):
-        hit = (landing[:, k : k + 1] == lane).astype(F32)
-        hit = jnp.broadcast_to(hit[:, None, :], (rows_dev, SUBLANES, lanes)).reshape(chunk, lanes)
-        turned = jnp.transpose(hit)[: n_sub * half_rows]
-        one_hot[:, k * chunk : (k + 1) * chunk] = turned.astype(jnp.bfloat16)
+        hit = (spread_landing[k : k + 1] == at_row).astype(F32)
+        one_hot[:, k * chunk : (k + 1) * chunk] = hit.astype(jnp.bfloat16)
 
     loads[0].wait()
 
@@ -129,39 +133,35 @@
 
     lax.fori_loop(0, rows_dev, turn, 0, unroll=4)
 
-    def pair_copy(e):
+    def block(e, slot, to_sub):
+        at = pl.multiple_of(to_sub * half_rows + slot * rows_dev, rows_dev)
+        return landed.at[e, pl.ds(at, rows_dev)]
+
+    def owner_copy(e, slot, step):
+        back = offsets.index(-offsets[slot] % n_rows)
+        where = corner(slot, step)
         return pltpu.make_async_remote_copy(
-            src_ref=landed.at[e, pl.ds(pl.multiple_of(twin * half_rows, rows_dev), half_rows)],
-            dst_ref=pair_recv.at[e],
-            send_sem=pair_send_sem.at[e],
-            recv_sem=pair_recv_sem.at[e],
-            device_id={"sub": twin},
+            src_ref=block(e, slot, where["sub"]),
+            dst_ref=recv.at[e, back, col, sub],
+            send_sem=send_sem.at[e, slot, step],
+            recv_sem=recv_sem.at[e, back, col, sub],
+            device_id=where,
             device_id_type=MESH,
         )
 
-    def owner_copy(e, slot, step):
-        back = offsets.index(-offsets[slot] % n_rows)
+    def owner_arrival(e, slot, step):
+        where = corner(slot, step)
         return pltpu.make_async_remote_copy(
-            src_ref=owned.at[e, pl.ds(slot * rows_dev, rows_dev)],
-            dst_ref=recv.at[e, back, col],
+            src_ref=block(e, slot, where["sub"]),
+            dst_ref=recv.at[e, slot, where["cols"], where["sub"]],
             send_sem=send_sem.at[e, slot, step],
-            recv_sem=recv_sem.at[e, back, col],
-            device_id={"rows": partner(slot), "cols": lax.rem(col + step, n_cols)},
+            recv_sem=recv_sem.at[e, slot, where["cols"], where["sub"]],
+            device_id=where,
             device_id_type=MESH,
         )
 
-    def owner_arrival(e, slot, step):
-        source = lax.rem(col + step, n_cols)
-        return pltpu.make_async_remote_copy(
-            src_ref=owned.at[e, pl.ds(slot * rows_dev, rows_dev)],
-            dst_ref=recv.at[e, slot, source],
-            send_sem=send_sem.at[e, slot, step],
-            recv_sem=recv_sem.at[e, slot, source],
-            device_id={"rows": partner(slot), "cols": source},
-            device_id_type=MESH,
-        )
-
-    routes = [(s, c) for s in range(slots) for c in range(n_cols) if (s, c) != (0, 0)]
+    far_first = sorted(range(slots), key=lambda s: -min(offsets[s], n_rows - offsets[s]))
+    routes = [(s, c) for s in far_first for c in reversed(range(n_cols * n_sub)) if (s, c) != (0, 0)]
 
     def each_route(act):
         for slot, step in routes:
@@ -170,7 +170,7 @@
     def dots_copy(e, step, peer, where):
         return pltpu.make_async_remote_copy(
             src_ref=dots.at[e],
-            dst_ref=dots_recv.at[e, me],
+            dst_ref=dots_recv.at[e, pl.ds(me, 1)],
             send_sem=dots_send_sem.at[e, step],
             recv_sem=dots_recv_sem.at[e, me],
             device_id=where,
@@ -178,25 +178,28 @@
         )
 
     def dots_start(e, products):
+        at = lax.broadcasted_iota(jnp.int32, (1, width), 1)
+        line = jnp.zeros((1, width), F32)
         for j, product in enumerate(products):
-            dots[e, j : j + 1] = jnp.sum(product, axis=0, keepdims=True)
+            total = jnp.sum(jnp.sum(product, axis=0, keepdims=True), axis=1, keepdims=True)
+            line = jnp.where(at == j, total, line)
+        dots[e] = line
         for step, peer, where in dot_peers():
             dots_copy(e, step, peer, where).start()
-        dots_recv[e, me] = dots[e]
+        dots_recv[e, pl.ds(me, 1)] = line
 
     def dots_finish(e, count):
         for step, peer, where in dot_peers():
             pltpu.make_async_remote_copy(
                 src_ref=dots.at[e],
-                dst_ref=dots_recv.at[e, peer],
+                dst_ref=dots_recv.at[e, pl.ds(peer, 1)],
                 send_sem=dots_send_sem.at[e, step],
                 recv_sem=dots_recv_sem.at[e, peer],
                 device_id=where,
                 device_id_type=MESH,
             ).wait_recv()
-        total = jnp.sum(dots_recv[e], axis=0)
-        total = jnp.broadcast_to(jnp.sum(total, axis=1, keepdims=True), total.shape)
-        return [total[j : j + 1] for j in range(count)]
+        total = jnp.sum(dots_recv[e], axis=0, keepdims=True)
+        return [jnp.broadcast_to(total[:, j : j + 1], total.shape) for j in range(count)]
 
     def fold(product):
         return jnp.sum(product.reshape(width // SUBLANES, SUBLANES, width), axis=0)
@@ -235,19 +238,16 @@
                 linked = 1
                 if offsets[slot] not in (0, n_rows // 2):
                     linked = (jnp.abs(partner(slot) - row) <= REACH).astype(jnp.int32)
-                greetings = greetings + (n_cols - 1) * linked
+                greetings = greetings + (n_cols - 1) * n_sub * linked
             pl.semaphore_wait(barrier, greetings)
-        pair_copy(e).start()
-        pair_copy(e).wait_recv()
-        mine = landed[e, pl.ds(pl.multiple_of(sub * half_rows, rows_dev), half_rows)]
-        owned[e] = mine + pair_recv[e]
         each_route(lambda slot, step: owner_copy(e, slot, step).start())
-        recv[e, 0, col] = owned[e, :rows_dev]
+        recv[e, 0, col, sub] = landed[e, pl.ds(pl.multiple_of(sub * half_rows, rows_dev), rows_dev)]
         own = jnp.sum(dprod[...].reshape(rows_dev, SUBLANES, width), axis=1)
         each_route(lambda slot, step: owner_arrival(e, slot, step).wait_recv())
         for slot in range(slots):
             for c in range(n_cols):
-                own = own + recv[e, slot, c]
+                for s in range(n_sub):
+                    own = own + recv[e, slot, c, s]
         return own
 
     shadow = right_ref[...]
@@ -289,14 +289,19 @@
     hat = jnp.transpose(hat)
     cross, square = dots_finish(3, 2)
     omega = cross / square
-    sol_ref[...] = hat[:rows_dev] + omega * hat[rows_dev : 2 * rows_dev]
-    res_ref[...] = half_next - omega * twice
+    out_ref[:rows_dev] = hat[:rows_dev] + omega * hat[rows_dev : 2 * rows_dev]
+    out_ref[rows_dev:] = half_next - omega * twice
 
     for e in range(APPLIES):
-        pair_copy(e).wait_send()
         each_route(lambda slot, step: owner_copy(e, slot, step).wait_send())
         for step, peer, where in dot_peers():
             dots_copy(e, step, peer, where).wait_send()
+
+
+def split(both_ref, sol_ref, res_ref):
+    rows_dev = sol_ref.shape[0]
+    sol_ref[...] = both_ref[:rows_dev]
+    res_ref[...] = both_ref[rows_dev:]
 
 
 def on_device(
@@ -320,31 +325,38 @@
         pltpu.VMEM((chunk, width), F32),
         pltpu.VMEM((APPLIES, rows_dev, width), F32),
         pltpu.VMEM((APPLIES, n_sub * half_rows, width), F32),
-        pltpu.VMEM((APPLIES, half_rows, width), F32),
-        pltpu.VMEM((APPLIES, half_rows, width), F32),
-        pltpu.VMEM((APPLIES, slots, n_cols, rows_dev, width), F32),
-        pltpu.VMEM((APPLIES, SUBLANES, width), F32),
-        pltpu.VMEM((APPLIES, peers, SUBLANES, width), F32),
+        pltpu.VMEM((APPLIES, slots, n_cols, n_sub, rows_dev, width), F32),
+        pltpu.VMEM((APPLIES, 1, width), F32),
+        pltpu.VMEM((APPLIES, peers, width), F32),
         dma((3,)),
-        dma((APPLIES,)),
-        dma((APPLIES,)),
-        dma((APPLIES, slots, n_cols)),
-        dma((APPLIES, slots, n_cols)),
+        dma((APPLIES, slots, n_cols * n_sub)),
+        dma((APPLIES, slots, n_cols, n_sub)),
         dma((APPLIES, peers)),
         dma((APPLIES, peers)),
     ]
-    out = jax.ShapeDtypeStruct(right_side.shape, F32)
-    return pl.pallas_call(
+    both = pl.pallas_call(
         functools.partial(kernel, (n_rows, n_cols, n_sub)),
-        out_shape=(out, out),
+        out_shape=jax.ShapeDtypeStruct((2 * rows_dev, width), F32),
         in_specs=[hbm, hbm, hbm, vmem, vmem, pl.BlockSpec(memory_space=pltpu.SMEM), vmem],
-        out_specs=(vmem, vmem),
+        out_specs=vmem,
         scratch_shapes=scratch,
         compiler_params=pltpu.CompilerParams(
             collective_id=0, has_side_effects=True, vmem_limit_bytes=56 * 2**20
         ),
         name="solve",
-    )(diagonal_tiles, coupling_tiles, jacobi_inverse, column_part, column_tile, neighbours, right_side)
+    )(
+        diagonal_tiles,
+        coupling_tiles,
+        jacobi_inverse,
+        column_part.T,
+        column_tile.T,
+        neighbours,
+        right_side,
+    )
+    out = jax.ShapeDtypeStruct(right_side.shape, F32)
+    return pl.pallas_call(
+        split, out_shape=(out, out), in_specs=[vmem], out_specs=(vmem, vmem), name="split"
+    )(both)
 
 
 def solution(mesh):

time: 41 us -> 35.2 us (0.86)
  local copies, waits for them, and re-layouts: 5.3 us -> 0 us
  Pallas kernels: 34.7 us -> 34.2 us
    unnamed x4 -> x0, local copies, waits for them, and re-layouts: 5.3 us -> none
    pallas_call x1, Pallas kernels: 34.7 us -> 32.9 us  [on_device(): pl.pallas_call(functools.partial(kernel, (n_rows, n_cols, n_sub)), out_sh...]
    pallas_call x0 -> x1, Pallas kernels: none -> 1.32 us  [on_device(): pl.pallas_call(split, out_shape=(out, out), in_specs=[vmem], out_specs=(v...]
where the time goes in v2:
time: 35.2 us; the launch traced here: 34.9 us
  Pallas kernels  34.2 us (97%)
  between operations  0.64 us (2%)
    pallas_call x1, Pallas kernels, on_device(): pl.pallas_call(functools.partial(kernel, (n_rows, n_cols, n_sub)), out_sh...  32.9 us
    pallas_call x1, Pallas kernels, on_device(): pl.pallas_call(split, out_shape=(out, out), in_specs=[vmem], out_specs=(v...  1.32 us

profile of v2, /device:TPU:0, one launch (start us, length us, event | category | flops | bytes accessed | tf_op | source)
XLA Modules:
  0.0 34.9 jit_solution(10322327252704864946)
XLA Ops:
  0.6 32.9 %solve.1.both_ref = f32[32,128]{1,0:T(8,128)} custom-call(f32[16,128,128]{2,1,0:T(8,128)} %diag_hbm.1, f32[16,3,128,128]{3,2,1,0:T(8,128)} %coup_hbm.1, f32[16,128,128]{2,1,0:T(8,128)} %jac_hbm.1, s32[3,16]{1,0:T(4,128)} %bitcast.2, s32[3,16]{1,0:T(4,128)} %bitcast.3, s32[4,4]{1,0:T(4,128)} %near_ref.1, f32[16,128]{1,0:T(8,128)} %right_ref.1), custom_call_target="tpu_custom_call" | custom-call | tf_op jit(solution)/shard_map/solve/pallas_call | solution.py:337
  33.6 1.3 %split.1 = (f32[16,128]{1,0:T(8,128)}, f32[16,128]{1,0:T(8,128)}) custom-call(f32[32,128]{1,0:T(8,128)} %solve.1.both_ref), custom_call_target="tpu_custom_call" | custom-call | tf_op jit(solution)/shard_map/split/pallas_call | solution.py:357

commit v3 on v2

--- a/solution.py
+++ b/solution.py
@@ -204,7 +204,7 @@
     def fold(product):
         return jnp.sum(product.reshape(width // SUBLANES, SUBLANES, width), axis=0)
 
-    unroll = 4 if rows_dev % 4 == 0 else 1
+    unroll = 8 if rows_dev % 8 == 0 else 1
 
     def apply(e, value):
         vec[e] = value

time: 35.2 us -> 34.5 us (0.980)
  Pallas kernels: 34.2 us -> 33.6 us
    pallas_call x1, Pallas kernels: 32.9 us -> 32.3 us  [on_device(): pl.pallas_call(functools.partial(kernel, (n_rows, n_cols, n_sub)), out_sh...]
where the time goes in v3:
time: 34.5 us; the launch traced here: 34.2 us
  Pallas kernels  33.6 us (97%)
  between operations  0.64 us (2%)
    pallas_call x1, Pallas kernels, on_device(): pl.pallas_call(functools.partial(kernel, (n_rows, n_cols, n_sub)), out_sh...  32.3 us
    pallas_call x1, Pallas kernels, on_device(): pl.pallas_call(split, out_shape=(out, out), in_specs=[vmem], out_specs=(v...  1.32 us

profile of v3, /device:TPU:0, one launch (start us, length us, event | category | flops | bytes accessed | tf_op | source)
XLA Modules:
  0.0 34.2 jit_solution(7243270526621961927)
XLA Ops:
  0.6 32.3 %solve.1.both_ref = f32[32,128]{1,0:T(8,128)} custom-call(f32[16,128,128]{2,1,0:T(8,128)} %diag_hbm.1, f32[16,3,128,128]{3,2,1,0:T(8,128)} %coup_hbm.1, f32[16,128,128]{2,1,0:T(8,128)} %jac_hbm.1, s32[3,16]{1,0:T(4,128)} %bitcast.2, s32[3,16]{1,0:T(4,128)} %bitcast.3, s32[4,4]{1,0:T(4,128)} %near_ref.1, f32[16,128]{1,0:T(8,128)} %right_ref.1), custom_call_target="tpu_custom_call" | custom-call | tf_op jit(solution)/shard_map/solve/pallas_call | solution.py:337
  32.9 1.3 %split.1 = (f32[16,128]{1,0:T(8,128)}, f32[16,128]{1,0:T(8,128)}) custom-call(f32[32,128]{1,0:T(8,128)} %solve.1.both_ref), custom_call_target="tpu_custom_call" | custom-call | tf_op jit(solution)/shard_map/split/pallas_call | solution.py:357
